TPU v7x, 32 devices: a whole 2x2x4 slice. The times are simulated.
32 devices in a mesh: grp: 4 (over x, core), mem: 8 (over z, y).
Axes of the slice: x: 2, y: 2, z: 4, core: 2. Of those that a mesh axis runs over, the one named last changes fastest.
Arguments:
- source_pts: float32 [64, 8192], P(None, ('grp', 'mem')), may hold values from -30 to 30
- target_pts: float32 [64, 8192], P(None, ('grp', 'mem')), may hold values from -30 to 30
- source_pot: float32 [8192], P(('grp', 'mem')), may hold values from -8 to 520
- target_pot: float32 [8192], P(('grp', 'mem')), may hold values from -8 to 520
- source_logw: float32 [8192], P(('grp', 'mem')), may hold values from -1 to 4
- target_logw: float32 [8192], P(('grp', 'mem')), may hold values from -1 to 4
Outputs:
- source_new: float32 [8192], P(('grp', 'mem'))
- target_new: float32 [8192], P(('grp', 'mem'))
All inputs are finite; a program needn't handle non-finite values.
Results may differ from a plain program's by a relative error of at most 0.0001.
Values sent between devices are 32-bit elements; how exact they have to be, the bound alone decides.
A program may use at most 64 MiB of HBM per device.

v0:
```python
import math

import jax
import jax.numpy as jnp
from jax import lax
from jax.sharding import PartitionSpec as P

epsilon = 4.0
floor_value = -1e30


def sweep(carry, points, squares, row_term, moving, offset):
    count = moving.shape[1]
    limit = 128
    width = math.gcd(count, limit)

    def block(index, state):
        row_max, row_sum, col_max, col_sum = state
        begin = index * width
        cols = lax.dynamic_slice_in_dim(moving, begin, width, 1)
        ycols = cols[:-1]
        cvals = cols[-1]
        ysq = 0.5 * jnp.sum(ycols * ycols, 0)
        cross = lax.dot_general(
            points,
            ycols,
            (((0,), (0,)), ((), ())),
            precision=lax.Precision.HIGHEST,
            preferred_element_type=jnp.float32,
        )
        half = (squares[:, None] + ysq[None, :] - cross) / epsilon
        scores = cvals[None, :] - half
        new_row = jnp.maximum(row_max, jnp.max(scores, 1))
        row_sum = row_sum * jnp.exp(row_max - new_row) + jnp.sum(
            jnp.exp(scores - new_row[:, None]), 1
        )
        others = row_term[:, None] - half
        place = offset + begin
        old_max = lax.dynamic_slice_in_dim(col_max, place, width, 0)
        old_sum = lax.dynamic_slice_in_dim(col_sum, place, width, 0)
        new_col = jnp.maximum(old_max, jnp.max(others, 0))
        new_sum = old_sum * jnp.exp(old_max - new_col) + jnp.sum(
            jnp.exp(others - new_col[None, :]), 0
        )
        col_max = lax.dynamic_update_slice_in_dim(col_max, new_col, place, 0)
        col_sum = lax.dynamic_update_slice_in_dim(col_sum, new_sum, place, 0)
        return (new_row, row_sum, col_max, col_sum)

    return lax.fori_loop(0, count // width, block, carry)


def totals(source_logw, target_logw):
    peaks = lax.pmax((jnp.max(source_logw), jnp.max(target_logw)), ("grp", "mem"))
    masses = lax.psum(
        (jnp.sum(jnp.exp(source_logw - peaks[0])), jnp.sum(jnp.exp(target_logw - peaks[1]))),
        ("grp", "mem"),
    )
    return (peaks[0] + jnp.log(masses[0]), peaks[1] + jnp.log(masses[1]))


def local(source_pts, target_pts, source_pot, target_pot, source_logw, target_logw):
    members = lax.axis_size("mem")
    rows = source_pts.shape[1]
    outer = rows * members
    src_norm, tgt_norm = totals(source_logw, target_logw)
    row_term = source_logw - src_norm + source_pot / epsilon
    col_term = target_logw - tgt_norm + target_pot / epsilon
    moving = jnp.concatenate([target_pts, col_term[None, :]], 0)
    standing = jnp.concatenate([source_pts, row_term[None, :]], 0)
    row_block = lax.all_gather(standing, "mem", axis=1, tiled=True)
    col_block = lax.all_gather(moving, "grp", axis=1, tiled=True)
    block_pts = row_block[:-1]
    block_terms = row_block[-1]
    block_sq = 0.5 * jnp.sum(block_pts * block_pts, 0)
    span = col_block.shape[1]
    carry = (
        jnp.full((outer,), floor_value, jnp.float32),
        jnp.zeros((outer,), jnp.float32),
        jnp.full((span,), floor_value, jnp.float32),
        jnp.zeros((span,), jnp.float32),
    )
    row_max, row_sum, col_max, col_sum = sweep(
        carry, block_pts, block_sq, block_terms, col_block, 0
    )
    rpeak = lax.pmax(row_max, "mem")
    own_rsum = lax.psum_scatter(
        row_sum * jnp.exp(row_max - rpeak), "mem", scatter_dimension=0, tiled=True
    )
    own_rmax = lax.dynamic_slice_in_dim(rpeak, lax.axis_index("mem") * rows, rows, 0)
    row_total = own_rmax + jnp.log(own_rsum)
    cpeak = lax.pmax(col_max, "grp")
    own_sum = lax.psum_scatter(
        col_sum * jnp.exp(col_max - cpeak), "grp", scatter_dimension=0, tiled=True
    )
    own_max = lax.dynamic_slice_in_dim(cpeak, lax.axis_index("grp") * rows, rows, 0)
    col_total = own_max + jnp.log(own_sum)
    row_hat = -epsilon * row_total
    col_hat = -epsilon * col_total
    return (0.5 * (source_pot + row_hat), 0.5 * (target_pot + col_hat))


def solution(mesh):
    return jax.shard_map(
        local,
        mesh=mesh,
        in_specs=(
            P(None, ("grp", "mem")),
            P(None, ("grp", "mem")),
            P(("grp", "mem")),
            P(("grp", "mem")),
            P(("grp", "mem")),
            P(("grp", "mem")),
        ),
        out_specs=(P(("grp", "mem")), P(("grp", "mem"))),
        check_vma=False,
    )
```

profile of v0, /device:TPU:0, one launch (start us, length us, event | category | flops | bytes accessed | tf_op | source)
XLA Modules:
  0.0 205.6 jit_solution(15678545301726195394)
XLA Ops:
  0.6 1.3 reduce_max.44
  1.9 0.6 reduce_max.45
  2.5 42.2 %all-reduce.3 = (f32[]{:T(128)}, f32[]{:T(128)}) all-reduce(f32[]{:T(128)} %reduce_max.44, f32[]{:T(128)} %reduce_max.45), channel_id=1, replica_groups=mesh['grp'=4,'mem'=8] {'grp','mem'}, use_global_device_ids=true, to_apply=%region_1.0 | all-reduce | flops 2 | bytes 16 | tf_op jit(solution)/shard_map/pmax | solution.py:53
  44.8 0.7 copy-done.3
  45.4 2.0 exponential_reduce_fusion.2
  47.4 40.6 %all-reduce.2 = (f32[]{:T(128)}, f32[]{:T(128)}) all-reduce(f32[]{:T(128)} %get-tuple-element.225, f32[]{:T(128)} %get-tuple-element.224), channel_id=1, replica_groups=mesh['grp'=4,'mem'=8] {'grp','mem'}, use_global_device_ids=true, to_apply=%region_3.0 | all-reduce | flops 2 | bytes 16 | tf_op jit(solution)/shard_map/psum | solution.py:54
  89.3 0.8 pad_maximum_fusion.1
  90.2 31.4 %all_gather.7 = f32[65,2048]{1,0:T(8,128)S(1)} all-gather(f32[65,256]{1,0:T(8,128)S(1)} %pad_maximum_fusion.1), channel_id=1, replica_groups=mesh['grp'=4,'mem'=8] {'mem'}, dimensions={1}, use_global_device_ids=true | all-gather | bytes 599040 | tf_op jit(solution)/shard_map/all_gather | solution.py:70
  121.7 0.7 copy-done
  123.8 6.7 %all_gather.6 = f32[65,1024]{1,0:T(8,128)S(1)} all-gather(f32[65,256]{1,0:T(8,128)S(1)} %pad_maximum_fusion), channel_id=1, replica_groups=mesh['grp'=4,'mem'=8] {'grp'}, dimensions={1}, use_global_device_ids=true | all-gather | bytes 332800 | tf_op jit(solution)/shard_map/all_gather | solution.py:71
  130.5 0.7 slice-done
  131.2 18.0 %while.20 = (s32[]{:T(128)}, f32[2048]{0:T(1024)S(1)}, f32[2048]{0:T(1024)S(1)}, f32[1024]{0:T(1024)S(1)}, f32[1024]{0:T(1024)S(1)}, /*index=5*/f32[65,1024]{1,0...) while((s32[]{:T(128)}, f32[2048]{0:T(1024)S(1)}, ...), condition=%wide.region_15.0_spmd.clone, body=%wide.region_9.0_spmd.clone.sunk | while | flops 204761344 | bytes 2844898 | solution.py:49
  131.2 1.3 subtract_reduce_fusion.3
  133.5 1.3 subtract_reduce_fusion.3
  135.7 1.3 subtract_reduce_fusion.3
  137.3 0.4 exponential_reduce_fusion.5
  138.0 1.3 subtract_reduce_fusion.3
  139.5 0.4 exponential_reduce_fusion.5
  140.2 1.3 subtract_reduce_fusion.3
  142.5 1.3 subtract_reduce_fusion.3
  144.8 1.3 subtract_reduce_fusion.3
  147.0 1.3 subtract_reduce_fusion.3
  149.2 7.1 %pmax.31 = f32[1024]{0:T(1024)S(1)} all-reduce(f32[1024]{0:T(1024)S(1)} %get-tuple-element.161), channel_id=1, replica_groups=mesh['grp'=4,'mem'=8] {'grp'}, use_global_device_ids=true, to_apply=%region_18.0 | all-reduce | flops 1024 | bytes 8192 | tf_op jit(solution)/shard_map/pmax | solution.py:91
  156.3 6.0 %all-reduce.1 = f32[1024]{0:T(1024)S(1)} all-reduce(f32[1024]{0:T(1024)S(1)} %exponential_multiply_fusion.1), channel_id=3, replica_groups=mesh['grp'=4,'mem'=8] {'grp'}, use_global_device_ids=true, to_apply=%region_19.0.clone | all-reduce | flops 1024 | bytes 8192
  162.3 0.6 copy-done.7
  162.9 0.6 dynamic-slice.2
  164.2 0.7 fusion.12
  164.8 20.8 %pmax.30 = f32[2048]{0:T(1024)S(1)} all-reduce(f32[2048]{0:T(1024)S(1)} %get-tuple-element.159), channel_id=1, replica_groups=mesh['grp'=4,'mem'=8] {'mem'}, use_global_device_ids=true, to_apply=%region_16.0 | all-reduce | flops 2048 | bytes 16384 | tf_op jit(solution)/shard_map/pmax | solution.py:85
  185.7 17.4 %all-reduce = f32[2048]{0:T(1024)S(1)} all-reduce(f32[2048]{0:T(1024)S(1)} %exponential_multiply_fusion), channel_id=2, replica_groups=mesh['grp'=4,'mem'=8] {'mem'}, use_global_device_ids=true, to_apply=%region_17.0.clone | all-reduce | flops 2048 | bytes 16384
  203.1 0.6 copy-done.6
  203.7 0.6 dynamic-slice
  205.0 0.7 fusion.11
  (110 shorter events, 6.3 us)
Async XLA Ops:
  0.6 1.3 copy-start.2
  44.8 0.7 copy-start.3
  88.6 0.7 copy-start.5
  121.6 0.8 copy-start
  121.6 2.1 %copy-start.1 = (f32[64,256]{1,0:T(8,128)S(1)}, f32[64,256]{1,0:T(8,128)}, u32[]{:S(2)}) copy-start(f32[64,256]{1,0:T(8,128)} %param.9) | copy-start | bytes 196612
  123.0 0.7 copy-start.4
  130.5 0.7 slice-start
  162.3 0.7 copy-start.7
  203.1 0.7 copy-start.6
where the time goes:
time: 206 us
  blocking collectives  172 us (83%)
  other arithmetic  13 us (6%)
  matrix products  10.4 us (5%)
  local copies, waits for them, and re-layouts  4.74 us (2%)
  between operations  4.67 us (2%)
    pmax x1, blocking collectives, totals(): lax.pmax((jnp.max(source_logw), jnp.max(target_logw)), ('grp', 'mem'))  42.2 us
    psum x1, blocking collectives, totals(): lax.psum((jnp.sum(jnp.exp(source_logw - peaks[0])), jnp.sum(jnp.exp(targe...  40.6 us
    all_gather x1, blocking collectives, local(): row_block = lax.all_gather(standing, 'mem', axis=1, tiled=True)  31.4 us
    unnamed x2, blocking collectives  23.4 us
    pmax x1, blocking collectives, local(): rpeak = lax.pmax(row_max, 'mem')  20.8 us
    dot_general x8, matrix products, block(): lax.dot_general(points, ycols, (((0,), (0,)), ((), ())), precision=lax.Pr...  10.4 us
    pmax x1, blocking collectives, local(): cpeak = lax.pmax(col_max, 'grp')  7.05 us
    all_gather x1, blocking collectives, local(): col_block = lax.all_gather(moving, 'grp', axis=1, tiled=True)  6.72 us

commit v1 on v0

v1 whole, which is shorter than its diff:
```python
import functools
import math

import jax
import jax.numpy as jnp
from jax import lax
from jax.experimental import pallas as pl
from jax.experimental.pallas import tpu as pltpu
from jax.sharding import PartitionSpec as P

MESH = pl.DeviceIdType.MESH
epsilon = 4.0
log2e = math.log2(math.e)
ln2 = math.log(2.0)


def inner_size(groups, members):
    inner = 1
    while members % inner or groups * inner < members // inner:
        inner += 1
    return inner


def split3(v):
    hi = v.astype(jnp.bfloat16)
    rest = v - hi.astype(jnp.float32)
    mid = rest.astype(jnp.bfloat16)
    low = (rest - mid.astype(jnp.float32)).astype(jnp.bfloat16)
    return hi, mid, low


def term_of(points, pot, logw):
    half = 0.5 * jnp.sum(points * points, 0, keepdims=True)
    return (logw + (pot - half) / epsilon) * log2e


def extra_rows(term, first):
    width = term.shape[1]
    hi, mid, low = (v.astype(jnp.float32) for v in split3(term))
    line = lax.broadcasted_iota(jnp.int32, (16, width), 0)
    base = 0 if first else 3
    ones = 3 - base
    out = jnp.where((line >= ones) & (line < ones + 3), 1.0, 0.0)
    for k, part in enumerate((hi, mid, low)):
        out = jnp.where(line == base + k, part, out)
    return out.astype(jnp.bfloat16)


def pack_left(points, pot, logw):
    hi, mid, low = split3(points * (log2e / epsilon))
    return jnp.concatenate(
        [hi, hi, mid, mid, hi, low, extra_rows(term_of(points, pot, logw), True)], 0
    )


def pack_right(points, pot, logw):
    hi, mid, low = split3(points)
    return jnp.concatenate(
        [hi, mid, hi, mid, low, hi, extra_rows(term_of(points, pot, logw), False)], 0
    )


def kernel(
    groups,
    inner,
    outer,
    x_ref,
    y_ref,
    xpot_ref,
    ypot_ref,
    xlog_ref,
    ylog_ref,
    xout_ref,
    yout_ref,
    xbuf,
    xpot,
    xlog,
    ybuf,
    ypot,
    ylog,
    ypack,
    cmax,
    csum,
    rowmsg,
    rowres,
    colmsg,
    colres,
    local_sem,
    xsend,
    xrecv,
    ysend,
    yrecv,
    rsend,
    rrecv,
    csend,
    crecv,
):
    plane = groups * inner
    rows = xbuf.shape[2]
    g = lax.axis_index("grp")
    mem = lax.axis_index("mem")
    z = mem // inner
    i = mem % inner
    me = g * inner + i

    def plane_dev(p):
        return (p // inner, z * inner + p % inner)

    def outer_dev(q):
        return (g, q * inner + i)

    xs = ((x_ref, xbuf), (xpot_ref, xpot), (xlog_ref, xlog))
    ys = ((y_ref, ybuf), (ypot_ref, ypot), (ylog_ref, ylog))
    locals_ = [
        pltpu.make_async_copy(src, dst.at[slot], local_sem.at[k])
        for k, (src, dst, slot) in enumerate(
            [(s, d, z) for s, d in ys] + [(s, d, me) for s, d in xs]
        )
    ]
    for c in locals_:
        c.start()

    barrier = pltpu.get_barrier_semaphore()
    for t in range(1, plane):
        pl.semaphore_signal(
            barrier, inc=1, device_id=plane_dev((me + t) % plane), device_id_type=MESH
        )
    for t in range(1, outer):
        pl.semaphore_signal(
            barrier, inc=1, device_id=outer_dev((z + t) % outer), device_id_type=MESH
        )
    for c in locals_:
        c.wait()
    pl.semaphore_wait(barrier, plane + outer - 2)

    def xcopy(k, slot, dest):
        dst = xs[k][1]
        return pltpu.make_async_remote_copy(
            src_ref=dst.at[slot],
            dst_ref=dst.at[slot],
            send_sem=xsend.at[k, dest],
            recv_sem=xrecv.at[k, slot],
            device_id=plane_dev(dest),
            device_id_type=MESH,
        )

    def ycopy(k, slot, dest):
        dst = ys[k][1]
        return pltpu.make_async_remote_copy(
            src_ref=dst.at[slot],
            dst_ref=dst.at[slot],
            send_sem=ysend.at[k, dest],
            recv_sem=yrecv.at[k, slot],
            device_id=outer_dev(dest),
            device_id_type=MESH,
        )

    def rowcopy(slot, dest):
        return pltpu.make_async_remote_copy(
            src_ref=rowmsg.at[dest],
            dst_ref=rowres.at[slot],
            send_sem=rsend.at[dest],
            recv_sem=rrecv.at[slot],
            device_id=plane_dev(dest),
            device_id_type=MESH,
        )

    def colcopy(slot, dest):
        return pltpu.make_async_remote_copy(
            src_ref=colmsg.at[dest],
            dst_ref=colres.at[slot],
            send_sem=csend.at[dest],
            recv_sem=crecv.at[slot],
            device_id=outer_dev(dest),
            device_id_type=MESH,
        )

    for t in range(1, outer):
        for k in range(3):
            ycopy(k, z, (z + t) % outer).start()
    for t in range(1, plane):
        for k in range(3):
            xcopy(k, me, (me + plane - t) % plane).start()

    def right_block(q):
        at = pl.ds(pl.multiple_of(q * rows, rows), rows)
        ypack[:, at] = pack_right(ybuf[q], ypot[q], ylog[q])

    right_block(z)
    for t in range(1, outer):
        q = (z + outer - t) % outer
        for k in range(3):
            ycopy(k, q, q).wait_recv()
        right_block(q)

    cmax[...] = jnp.full(cmax.shape, -3e38, jnp.float32)
    csum[...] = jnp.zeros(csum.shape, jnp.float32)
    tlog = jnp.concatenate([ylog[q] for q in range(outer)], 1)
    tpeak = jnp.max(tlog)
    tmass = jnp.sum(jnp.exp(tlog - tpeak))
    lane = lax.broadcasted_iota(jnp.int32, (rows, 128), 1)

    def step(t, _):
        p = (me + t) % plane

        @pl.when(t > 0)
        def _():
            for k in range(3):
                xcopy(k, p, p).wait_recv()

        left = pack_left(xbuf[p], xpot[p], xlog[p])
        scores = lax.dot_general(
            left,
            ypack[...],
            (((0,), (0,)), ((), ())),
            preferred_element_type=jnp.float32,
        )
        peak = jnp.max(scores, 1, keepdims=True)
        mass = jnp.sum(jnp.exp2(scores - peak), 1, keepdims=True)
        tall = scores.reshape(rows // 8, 8, scores.shape[1])
        new = jnp.maximum(cmax[...], jnp.max(tall, 0))
        csum[...] = csum[...] * jnp.exp2(cmax[...] - new) + jnp.sum(
            jnp.exp2(tall - new[None]), 0
        )
        cmax[...] = new
        tile = jnp.where(
            lane == 0, peak, jnp.where(lane == 1, mass, jnp.where(lane == 2, tpeak, tmass))
        )
        msg = tile.T[:8]

        @pl.when(t > 0)
        def _():
            rowmsg[p] = msg
            rowcopy(me, p).start()

        @pl.when(t == 0)
        def _():
            rowres[me] = msg

        return 0

    lax.fori_loop(0, plane, step, 0)

    slog = jnp.concatenate([xlog[p] for p in range(plane)], 1)
    speak = jnp.max(slog)
    smass = jnp.sum(jnp.exp(slog - speak))
    peak = jnp.max(cmax[...], 0, keepdims=True)
    mass = jnp.sum(csum[...] * jnp.exp2(cmax[...] - peak), 0, keepdims=True)
    line = lax.broadcasted_iota(jnp.int32, (8, rows), 0)

    for q in range(outer):
        part = slice(q * rows, (q + 1) * rows)
        colmsg[q] = jnp.where(
            line == 0,
            peak[:, part],
            jnp.where(line == 1, mass[:, part], jnp.where(line == 2, speak, smass)),
        )
    for t in range(1, outer):
        colcopy(z, (z + t) % outer).start()
    colres[z] = colmsg[z]

    def combine(res, pot, logw):
        peaks = res[:, 0:1]
        top = jnp.max(peaks, 0)
        total = jnp.sum(res[:, 1:2] * jnp.exp2(peaks - top[None]), 0)
        lse = ln2 * (top + jnp.log2(total))
        wpeaks = res[:, 2:3]
        wtop = jnp.max(wpeaks, 0)
        wtotal = jnp.sum(res[:, 3:4] * jnp.exp(wpeaks - wtop[None]), 0)
        norm = wtop + jnp.log(wtotal)
        hat = -epsilon * (lse - logw - pot / epsilon - norm)
        return 0.5 * (pot + hat)

    for t in range(1, plane):
        p = (me + plane - t) % plane
        rowcopy(p, p).wait_recv()
    xout_ref[...] = combine(rowres[...], xpot[me], xlog[me])
    for t in range(1, outer):
        q = (z + outer - t) % outer
        colcopy(q, q).wait_recv()
    yout_ref[...] = combine(colres[...], ypot[z], ylog[z])

    for t in range(1, outer):
        q = (z + t) % outer
        for k in range(3):
            ycopy(k, z, q).wait_send()
        colcopy(z, q).wait_send()
    for t in range(1, plane):
        p = (me + t) % plane
        for k in range(3):
            xcopy(k, me, p).wait_send()
        rowcopy(me, p).wait_send()


def local(groups, members, x, y, xpot, ypot, xlog, ylog):
    inner = inner_size(groups, members)
    outer = members // inner
    plane = groups * inner
    feat, rows = x.shape
    span = outer * rows
    depth = 6 * feat + 16
    f32 = jnp.float32
    dma = pltpu.SemaphoreType.DMA
    out = pl.pallas_call(
        functools.partial(kernel, groups, inner, outer),
        out_shape=(jax.ShapeDtypeStruct((1, rows), f32),) * 2,
        in_specs=[pl.BlockSpec(memory_space=pl.ANY)] * 6,
        out_specs=(pl.BlockSpec(memory_space=pltpu.VMEM),) * 2,
        scratch_shapes=[
            pltpu.VMEM((plane, feat, rows), f32),
            pltpu.VMEM((plane, 1, rows), f32),
            pltpu.VMEM((plane, 1, rows), f32),
            pltpu.VMEM((outer, feat, rows), f32),
            pltpu.VMEM((outer, 1, rows), f32),
            pltpu.VMEM((outer, 1, rows), f32),
            pltpu.VMEM((depth, span), jnp.bfloat16),
            pltpu.VMEM((8, span), f32),
            pltpu.VMEM((8, span), f32),
            pltpu.VMEM((plane, 8, rows), f32),
            pltpu.VMEM((plane, 8, rows), f32),
            pltpu.VMEM((outer, 8, rows), f32),
            pltpu.VMEM((outer, 8, rows), f32),
            dma((6,)),
            dma((3, plane)),
            dma((3, plane)),
            dma((3, outer)),
            dma((3, outer)),
            dma((plane,)),
            dma((plane,)),
            dma((outer,)),
            dma((outer,)),
        ],
        compiler_params=pltpu.CompilerParams(collective_id=0, has_side_effects=True),
        name="sinkhorn",
    )(x, y, *(v.reshape(1, rows) for v in (xpot, ypot, xlog, ylog)))
    return tuple(v.reshape(rows) for v in out)


def solution(mesh):
    both = ("grp", "mem")
    return jax.shard_map(
        functools.partial(local, mesh.shape["grp"], mesh.shape["mem"]),
        mesh=mesh,
        in_specs=(P(None, both), P(None, both), P(both), P(both), P(both), P(both)),
        out_specs=(P(both), P(both)),
        check_vma=False,
    )
```

time: 206 us -> 27.7 us (0.13)
  blocking collectives: 172 us -> 0 us
  Pallas kernels: 0 us -> 25 us
  other arithmetic: 13 us -> 0 us
  matrix products: 10.4 us -> 0 us
  between operations: 4.67 us -> 0.65 us
  local copies, waits for them, and re-layouts: 4.74 us -> 1.86 us
    pmax x3 -> x0, blocking collectives: 70.1 us -> none  [the longest x1 42.2 us: totals(): lax.pmax((jnp.max(source_logw), jnp.max(target_logw)), ('grp', 'mem'))]
    psum x1 -> x0, blocking collectives: 40.6 us -> none  [totals(): lax.psum((jnp.sum(jnp.exp(source_logw - peaks[0])), jnp.sum(jnp.exp(targe...]
    all_gather x2 -> x0, blocking collectives: 38.2 us -> none  [the longest x1 31.4 us: local(): row_block = lax.all_gather(standing, 'mem', axis=1, tiled=True)]
    pallas_call x0 -> x1, Pallas kernels: none -> 25 us  [local(): pl.pallas_call(functools.partial(kernel, groups, inner, outer), out_shape...]
    unnamed x2 -> x0, blocking collectives: 23.4 us -> none
    dot_general x8 -> x0, matrix products: 10.4 us -> none  [block(): lax.dot_general(points, ycols, (((0,), (0,)), ((), ())), precision=lax.Pr...]
    reduce_sum x17 -> x0, other arithmetic: 5.7 us -> none  [the longest x8 3.46 us: block(): jnp.sum(jnp.exp(others - new_col[None, :]), 0)]
    dynamic_update_slice x16 -> x0, other arithmetic: 2.96 us -> none  [the longest x8 1.49 us: block(): col_max = lax.dynamic_update_slice_in_dim(col_max, new_col, place, 0)]
where the time goes in v1:
time: 27.7 us; the launch traced here: 27.5 us
  Pallas kernels  25 us (90%)
  local copies, waits for them, and re-layouts  1.86 us (7%)
  between operations  0.65 us (2%)
    pallas_call x1, Pallas kernels, local(): pl.pallas_call(functools.partial(kernel, groups, inner, outer), out_shape...  25 us
    unnamed x6, local copies, waits for them, and re-layouts  1.86 us

profile of v1, /device:TPU:0, one launch (start us, length us, event | category | flops | bytes accessed | tf_op | source)
XLA Modules:
  0.0 27.5 jit_solution(10226681227604881377)
XLA Ops:
  0.6 25.0 %sinkhorn.1 = (f32[1,256]{1,0:T(1,128)}, f32[1,256]{1,0:T(1,128)}) custom-call(f32[64,256]{1,0:T(8,128)} %x_ref.1, f32[64,256]{1,0:T(8,128)} %y_ref.1, f32[1,256]{1,0:T(1,128)} %bitcast.6, f32[1,256]{1,0:T(1,128)} %bitcast.7, f32[1,256]{1,0:T(1,128)} %bitcast.8, f32[1,256]{1,0:T(1,128)} %bitcast.9), custom_call_target="tpu_custom_call" | custom-call | tf_op jit(solution)/shard_map/sinkhorn/pallas_call | solution.py:304
  25.7 0.0 copy-start.1
  25.7 0.7 %copy-done.1 = f32[1,256]{1,0:T(1,128)S(1)} copy-done((f32[1,256]{1,0:T(1,128)S(1)}, f32[1,256]{1,0:T(1,128)}, u32[]{:S(2)}) %copy-start.1) | copy-done | bytes 1048
  26.3 0.0 copy-start
  26.3 0.6 %copy.10 = f32[256]{0:T(256)} copy(f32[256]{0:T(256)S(1)} %bitcast.11) | data formatting | bytes 2048
  26.9 0.1 copy-done
  27.0 0.6 %copy.11 = f32[256]{0:T(256)} copy(f32[256]{0:T(256)S(1)} %bitcast.10) | data formatting | bytes 2048
Async XLA Ops:
  25.7 0.7 %copy-start.1 = (f32[1,256]{1,0:T(1,128)S(1)}, f32[1,256]{1,0:T(1,128)}, u32[]{:S(2)}) copy-start(f32[1,256]{1,0:T(1,128)} %get-tuple-element.4) | copy-start | bytes 3076
  26.3 0.6 %copy-start = (f32[1,256]{1,0:T(1,128)S(1)}, f32[1,256]{1,0:T(1,128)}, u32[]{:S(2)}) copy-start(f32[1,256]{1,0:T(1,128)} %get-tuple-element.5) | copy-start | bytes 3076

commit v2 on v1

--- a/solution.py
+++ b/solution.py
@@ -79,6 +79,7 @@
     ypot,
     ylog,
     ypack,
+    lpack,
     cmax,
     csum,
     rowmsg,
@@ -95,6 +96,8 @@
     csend,
     crecv,
 ):
+    chunks = 2 - outer % 2
+    half = outer // chunks
     plane = groups * inner
     rows = xbuf.shape[2]
     g = lax.axis_index("grp")
@@ -155,12 +158,12 @@
             device_id_type=MESH,
         )
 
-    def rowcopy(slot, dest):
+    def rowcopy(chunk, slot, dest):
         return pltpu.make_async_remote_copy(
-            src_ref=rowmsg.at[dest],
-            dst_ref=rowres.at[slot],
-            send_sem=rsend.at[dest],
-            recv_sem=rrecv.at[slot],
+            src_ref=rowmsg.at[chunk * plane + dest],
+            dst_ref=rowres.at[chunk * plane + slot],
+            send_sem=rsend.at[chunk * plane + dest],
+            recv_sem=rrecv.at[chunk * plane + slot],
             device_id=plane_dev(dest),
             device_id_type=MESH,
         )
@@ -175,71 +178,86 @@
             device_id_type=MESH,
         )
 
-    for t in range(1, outer):
-        for k in range(3):
-            ycopy(k, z, (z + t) % outer).start()
+    def block_of(chunk, t):
+        return (z // half + chunk) % chunks * half + (z + t) % half
+
+    for chunk in range(chunks):
+        for t in range(chunk == 0, half):
+            for k in range(3):
+                ycopy(k, z, block_of(chunk, t)).start()
     for t in range(1, plane):
         for k in range(3):
             xcopy(k, me, (me + plane - t) % plane).start()
 
-    def right_block(q):
-        at = pl.ds(pl.multiple_of(q * rows, rows), rows)
-        ypack[:, at] = pack_right(ybuf[q], ypot[q], ylog[q])
-
-    right_block(z)
-    for t in range(1, outer):
-        q = (z + outer - t) % outer
-        for k in range(3):
-            ycopy(k, q, q).wait_recv()
-        right_block(q)
-
     cmax[...] = jnp.full(cmax.shape, -3e38, jnp.float32)
     csum[...] = jnp.zeros(csum.shape, jnp.float32)
-    tlog = jnp.concatenate([ylog[q] for q in range(outer)], 1)
-    tpeak = jnp.max(tlog)
-    tmass = jnp.sum(jnp.exp(tlog - tpeak))
     lane = lax.broadcasted_iota(jnp.int32, (rows, 128), 1)
 
-    def step(t, _):
-        p = (me + t) % plane
-
-        @pl.when(t > 0)
-        def _():
-            for k in range(3):
-                xcopy(k, p, p).wait_recv()
-
-        left = pack_left(xbuf[p], xpot[p], xlog[p])
-        scores = lax.dot_general(
-            left,
-            ypack[...],
-            (((0,), (0,)), ((), ())),
-            preferred_element_type=jnp.float32,
-        )
-        peak = jnp.max(scores, 1, keepdims=True)
-        mass = jnp.sum(jnp.exp2(scores - peak), 1, keepdims=True)
-        tall = scores.reshape(rows // 8, 8, scores.shape[1])
-        new = jnp.maximum(cmax[...], jnp.max(tall, 0))
-        csum[...] = csum[...] * jnp.exp2(cmax[...] - new) + jnp.sum(
-            jnp.exp2(tall - new[None]), 0
-        )
-        cmax[...] = new
-        tile = jnp.where(
-            lane == 0, peak, jnp.where(lane == 1, mass, jnp.where(lane == 2, tpeak, tmass))
-        )
-        msg = tile.T[:8]
-
-        @pl.when(t > 0)
-        def _():
-            rowmsg[p] = msg
-            rowcopy(me, p).start()
-
-        @pl.when(t == 0)
-        def _():
-            rowres[me] = msg
-
-        return 0
-
-    lax.fori_loop(0, plane, step, 0)
+    for chunk in range(chunks):
+        logs = []
+        for t in range(half):
+            q = block_of(chunk, t)
+            if chunk or t:
+                for k in range(3):
+                    ycopy(k, q, q).wait_recv()
+            at = pl.ds(pl.multiple_of(q * rows, rows), rows)
+            ypack[:, at] = pack_right(ybuf[q], ypot[q], ylog[q])
+            logs.append(ylog[q])
+        tlog = jnp.concatenate(logs, 1)
+        tpeak = jnp.max(tlog)
+        tmass = jnp.sum(jnp.exp(tlog - tpeak))
+        width = half * rows
+        begin = (z // half + chunk) % chunks * width
+        cols = pl.ds(pl.multiple_of(begin, rows), width)
+
+        def step(t, _, chunk=chunk, tpeak=tpeak, tmass=tmass, cols=cols):
+            p = (me + t) % plane
+
+            if chunk == 0:
+
+                @pl.when(t > 0)
+                def _():
+                    for k in range(3):
+                        xcopy(k, p, p).wait_recv()
+
+                left = pack_left(xbuf[p], xpot[p], xlog[p])
+                lpack[p] = left
+            else:
+                left = lpack[p]
+            scores = lax.dot_general(
+                left,
+                ypack[:, cols],
+                (((0,), (0,)), ((), ())),
+                preferred_element_type=jnp.float32,
+            )
+            peak = jnp.max(scores, 1, keepdims=True)
+            mass = jnp.sum(jnp.exp2(scores - peak), 1, keepdims=True)
+            tall = scores.reshape(rows // 8, 8, scores.shape[1])
+            old = cmax[:, cols]
+            new = jnp.maximum(old, jnp.max(tall, 0))
+            csum[:, cols] = csum[:, cols] * jnp.exp2(old - new) + jnp.sum(
+                jnp.exp2(tall - new[None]), 0
+            )
+            cmax[:, cols] = new
+            tile = jnp.where(
+                lane == 0,
+                peak,
+                jnp.where(lane == 1, mass, jnp.where(lane == 2, tpeak, tmass)),
+            )
+            msg = tile.T[:8]
+
+            @pl.when(t > 0)
+            def _():
+                rowmsg[chunk * plane + p] = msg
+                rowcopy(chunk, me, p).start()
+
+            @pl.when(t == 0)
+            def _():
+                rowres[chunk * plane + me] = msg
+
+            return 0
+
+        lax.fori_loop(0, plane, step, 0)
 
     slog = jnp.concatenate([xlog[p] for p in range(plane)], 1)
     speak = jnp.max(slog)
@@ -268,12 +286,12 @@
         wtop = jnp.max(wpeaks, 0)
         wtotal = jnp.sum(res[:, 3:4] * jnp.exp(wpeaks - wtop[None]), 0)
         norm = wtop + jnp.log(wtotal)
-        hat = -epsilon * (lse - logw - pot / epsilon - norm)
-        return 0.5 * (pot + hat)
+        return -epsilon * (lse - logw - pot / epsilon - norm)
 
     for t in range(1, plane):
         p = (me + plane - t) % plane
-        rowcopy(p, p).wait_recv()
+        for chunk in range(chunks):
+            rowcopy(chunk, p, p).wait_recv()
     xout_ref[...] = combine(rowres[...], xpot[me], xlog[me])
     for t in range(1, outer):
         q = (z + outer - t) % outer
@@ -289,12 +307,14 @@
         p = (me + t) % plane
         for k in range(3):
             xcopy(k, me, p).wait_send()
-        rowcopy(me, p).wait_send()
+        for chunk in range(chunks):
+            rowcopy(chunk, me, p).wait_send()
 
 
 def local(groups, members, x, y, xpot, ypot, xlog, ylog):
     inner = inner_size(groups, members)
     outer = members // inner
+    chunks = 2 - outer % 2
     plane = groups * inner
     feat, rows = x.shape
     span = outer * rows
@@ -314,10 +334,11 @@
             pltpu.VMEM((outer, 1, rows), f32),
             pltpu.VMEM((outer, 1, rows), f32),
             pltpu.VMEM((depth, span), jnp.bfloat16),
+            pltpu.VMEM((plane, depth, rows), jnp.bfloat16),
             pltpu.VMEM((8, span), f32),
             pltpu.VMEM((8, span), f32),
-            pltpu.VMEM((plane, 8, rows), f32),
-            pltpu.VMEM((plane, 8, rows), f32),
+            pltpu.VMEM((chunks * plane, 8, rows), f32),
+            pltpu.VMEM((chunks * plane, 8, rows), f32),
             pltpu.VMEM((outer, 8, rows), f32),
             pltpu.VMEM((outer, 8, rows), f32),
             dma((6,)),
@@ -325,15 +346,15 @@
             dma((3, plane)),
             dma((3, outer)),
             dma((3, outer)),
-            dma((plane,)),
-            dma((plane,)),
+            dma((chunks * plane,)),
+            dma((chunks * plane,)),
             dma((outer,)),
             dma((outer,)),
         ],
         compiler_params=pltpu.CompilerParams(collective_id=0, has_side_effects=True),
         name="sinkhorn",
     )(x, y, *(v.reshape(1, rows) for v in (xpot, ypot, xlog, ylog)))
-    return tuple(v.reshape(rows) for v in out)
+    return tuple(0.5 * (pot + v.reshape(rows)) for v, pot in zip(out, (xpot, ypot)))
 
 
 def solution(mesh):

time: 27.7 us -> 28.3 us (1.022)
  Pallas kernels: 25 us -> 26.2 us
  local copies, waits for them, and re-layouts: 1.86 us -> 0.68 us
  other arithmetic: 0 us -> 0.57 us
    unnamed x6 -> x8, local copies, waits for them, and re-layouts: 1.86 us -> 0.68 us
    pallas_call x1, Pallas kernels: 25 us -> 26.2 us  [local(): pl.pallas_call(functools.partial(kernel, groups, inner, outer), out_shape...]
    mul x0 -> x1, other arithmetic: none -> 0.57 us  [local(): 0.5 * (pot + v.reshape(rows))]
where the time goes in v2:
time: 28.3 us; the launch traced here: 28.1 us
  Pallas kernels  26.2 us (93%)
  local copies, waits for them, and re-layouts  0.68 us (2%)
  between operations  0.67 us (2%)
  other arithmetic  0.57 us (2%)
    pallas_call x1, Pallas kernels, local(): pl.pallas_call(functools.partial(kernel, groups, inner, outer), out_shape...  26.2 us
    unnamed x8, local copies, waits for them, and re-layouts  0.68 us
    mul x1, other arithmetic, local(): 0.5 * (pot + v.reshape(rows))  0.57 us

profile of v2, /device:TPU:0, one launch (start us, length us, event | category | flops | bytes accessed | tf_op | source)
XLA Modules:
  0.0 28.1 jit_solution(1442054030911668008)
XLA Ops:
  0.6 26.2 %sinkhorn.1 = (f32[1,256]{1,0:T(1,128)}, f32[1,256]{1,0:T(1,128)}) custom-call(f32[64,256]{1,0:T(8,128)} %x_ref.1, f32[64,256]{1,0:T(8,128)} %y_ref.1, f32[1,256]{1,0:T(1,128)} %bitcast.7, f32[1,256]{1,0:T(1,128)} %bitcast.6, f32[1,256]{1,0:T(1,128)} %bitcast.8, f32[1,256]{1,0:T(1,128)} %bitcast.9), custom_call_target="tpu_custom_call" | custom-call | tf_op jit(solution)/shard_map/sinkhorn/pallas_call | solution.py:324
  26.8 0.0 copy-start.3
  26.8 0.0 copy-start.1
  26.8 0.0 copy-start.2
  26.8 0.0 copy-start
  26.9 0.6 %copy-done.3 = f32[1,256]{1,0:T(1,128)S(1)} copy-done((f32[1,256]{1,0:T(1,128)S(1)}, f32[1,256]{1,0:T(1,128)}, u32[]{:S(2)}) %copy-start.3) | copy-done | bytes 1048
  27.5 0.0 copy-done.1
  27.5 0.0 copy-done.2
  27.5 0.0 copy-done
  27.5 0.6 %add_multiply_fusion = (f32[256]{0:T(256)}, f32[256]{0:T(256)}) fusion(f32[256]{0:T(256)S(1)} %copy-done, f32[256]{0:T(256)S(1)} %bitcast.11, f32[256]{0:T(256)S(1)} %copy-done.1, f32[256]{0:T(256)S(1)} %bitcast.10), kind=kLoop, calls=%fused_computation | loop fusion | flops 1024 | bytes 6144 | tf_op jit(solution)/shard_map/mul | solution.py:357
Async XLA Ops:
  26.8 0.7 %copy-start.3 = (f32[1,256]{1,0:T(1,128)S(1)}, f32[1,256]{1,0:T(1,128)}, u32[]{:S(2)}) copy-start(f32[1,256]{1,0:T(1,128)} %get-tuple-element.5) | copy-start | bytes 3076
  26.8 0.7 %copy-start.1 = (f32[256]{0:T(256)S(1)}, f32[256]{0:T(256)}, u32[]{:S(2)}) copy-start(f32[256]{0:T(256)} %param.8) | copy-start | bytes 3076
  26.8 0.7 %copy-start.2 = (f32[1,256]{1,0:T(1,128)S(1)}, f32[1,256]{1,0:T(1,128)}, u32[]{:S(2)}) copy-start(f32[1,256]{1,0:T(1,128)} %get-tuple-element.4) | copy-start | bytes 3076
  26.8 0.7 %copy-start = (f32[256]{0:T(256)S(1)}, f32[256]{0:T(256)}, u32[]{:S(2)}) copy-start(f32[256]{0:T(256)} %param.9) | copy-start | bytes 3076
